TPU v7x, 32 devices: a whole 2x2x4 slice. The times are simulated.
32 devices in a mesh: ens: 2 (over y), gy: 4 (over z), gx: 4 (over x, core).
Axes of the slice: x: 2, y: 2, z: 4, core: 2. Of those that a mesh axis runs over, the one named last changes fastest.
Arguments:
- velocity: float32 [2, 2, 1024, 1024], P('ens', None, 'gy', 'gx'), may hold values from -3 to 3
- stress: float32 [2, 3, 1024, 1024], P('ens', None, 'gy', 'gx'), may hold values from -3 to 3
- thickness: float32 [2, 1024, 1024], P('ens', 'gy', 'gx'), may hold values from 2 to 3
- concentration: float32 [2, 1024, 1024], P('ens', 'gy', 'gx'), may hold values from 0.97 to 1
- node_mass: float32 [2, 1024, 1024], P('ens', 'gy', 'gx'), may hold values from 1 to 1.5
- wind_stress: float32 [2, 2, 1024, 1024], P('ens', None, 'gy', 'gx'), may hold values from -3 to 3
- ocean_current: float32 [2, 2, 1024, 1024], P('ens', None, 'gy', 'gx'), may hold values from -2 to 2
- ocean_mask: int32 [1024, 1024], P('gy', 'gx'), may hold values 0 or 1
- ice_blocks: int32 [2, 32, 32], P('ens', 'gy', 'gx'), may hold values 0 or 1
Outputs:
- velocity_out: float32 [2, 2, 1024, 1024], P('ens', None, 'gy', 'gx')
- stress_out: float32 [2, 3, 1024, 1024], P('ens', None, 'gy', 'gx')
- ensemble_mean: float32 [3, 1024, 1024], P(None, ('gy', 'ens'), 'gx')
- ensemble_variance: float32 [3, 1024, 1024], P(None, ('gy', 'ens'), 'gx')
All inputs are finite; a program needn't handle non-finite values. No bound on the sum of `ocean_mask` or of `ice_blocks` on one device may be relied on, other than what follows from the above.
Results may differ from a plain program's by a relative error of at most 0.00002.
Values sent between devices are 32-bit elements; how exact they have to be, the bound alone decides.
A program may use at most 64 MiB of HBM per device.

v0:
```python
import functools

import jax
import jax.numpy as jnp
from jax import lax
from jax.experimental import pallas as pl
from jax.experimental.pallas import tpu as pltpu
from jax.sharding import PartitionSpec as P

SUBCYCLES = 16
BLOCK = 32

TIME_STEP = 0.5
RELAX_RATE = 0.25
ECCENTRICITY_SQUARED = 4.0
DELTA_FLOOR = 0.5
CORIOLIS_TOP = 1.0
STRENGTH_DECAY = 20.0

MESH = pl.DeviceIdType.MESH
LANES = 128
MARGIN = SUBCYCLES
EXTRA = 8
WIDE = 18
FIELDS = 12
PER_TILE = LANES // WIDE
X_TILES = -(-FIELDS // PER_TILE)
PER_CORNER = LANES // (2 * WIDE)
C_TILES = -(-FIELDS // PER_CORNER)
TOP = 8
STEP = 32
TINY = 1.1754944e-38


def lane_index(rows):
    return lax.broadcasted_iota(jnp.int32, (rows, LANES), 1)


def rolled(value, shift):
    shift = shift % LANES
    return value if shift == 0 else pltpu.roll(value, shift, 1)


def exchange_kernel(
    sizes,
    vel, stress, thick, conc, mass, wind, cur, mask, ice,
    derived, halo, rows_lo, rows_hi,
    x_out, x_in, y_up, y_dn, in_hi, in_lo, c_up, c_dn, cin_hi, cin_lo,
    send_sem, recv_sem,
):
    gx_count, gy_count = sizes
    rows, cols = thick.shape
    gx, gy = lax.axis_index("gx"), lax.axis_index("gy")
    right, left = lax.rem(gx + 1, gx_count), lax.rem(gx + gx_count - 1, gx_count)
    has_lo, has_hi = gy > 0, gy < gy_count - 1
    lower, upper = jnp.maximum(gy - 1, 0), jnp.minimum(gy + 1, gy_count - 1)

    barrier = pltpu.get_barrier_semaphore()
    for side in (left, right):
        pl.semaphore_signal(barrier, inc=1, device_id={"gx": side}, device_id_type=MESH)

    @pl.when(has_lo)
    def _():
        pl.semaphore_signal(barrier, inc=1, device_id={"gy": lower}, device_id_type=MESH)

    @pl.when(has_hi)
    def _():
        pl.semaphore_signal(barrier, inc=1, device_id={"gy": upper}, device_id_type=MESH)

    block_rows, block_cols = ice.shape
    spread_rows = (
        lax.broadcasted_iota(jnp.int32, (rows, block_rows), 0) // BLOCK
        == lax.broadcasted_iota(jnp.int32, (rows, block_rows), 1)
    ).astype(jnp.float32)
    spread_cols = (
        lax.broadcasted_iota(jnp.int32, (block_cols, cols), 1) // BLOCK
        == lax.broadcasted_iota(jnp.int32, (block_cols, cols), 0)
    ).astype(jnp.float32)
    present = jnp.dot(
        jnp.dot(spread_rows, ice[...].astype(jnp.float32), preferred_element_type=jnp.float32),
        spread_cols,
        preferred_element_type=jnp.float32,
    )
    derived[0] = thick[...] * jnp.exp(-STRENGTH_DECAY * (1.0 - conc[...]))
    derived[1] = mask[...].astype(jnp.float32) * present

    def field(f, r, c):
        if f < 2:
            return vel[f, r, c] * derived[1, r, c]
        if f < 5:
            return stress[f - 2, r, c]
        if f == 5:
            return derived[0, r, c]
        if f == 6:
            return mass[r, c]
        if f < 9:
            return wind[f - 7, r, c]
        if f < 11:
            return cur[f - 9, r, c]
        return derived[1, r, c]

    every = slice(0, rows)
    lanes = lane_index(rows)
    first, last = slice(0, LANES), slice(cols - LANES, cols)
    for tile in range(X_TILES):
        east = jnp.zeros((rows, LANES), jnp.float32)
        west = jnp.zeros((rows, LANES), jnp.float32)
        for f in range(tile * PER_TILE, min(FIELDS, (tile + 1) * PER_TILE)):
            at = (f - tile * PER_TILE) * WIDE
            here = jnp.logical_and(lanes >= at, lanes < at + WIDE)
            east = jnp.where(here, rolled(field(f, every, last), at - (LANES - WIDE)), east)
            west = jnp.where(here, rolled(field(f, every, first), at), west)
        x_out[0, tile] = east
        x_out[1, tile] = west
    wide = slice(0, cols)
    for f in range(FIELDS):
        at = slice(f * MARGIN, (f + 1) * MARGIN)
        y_up[at] = field(f, slice(0, MARGIN), wide)
        y_dn[at] = field(f, slice(rows - MARGIN, rows), wide)
    for f in range(2):
        at = FIELDS * MARGIN + f * EXTRA
        y_up[at : at + EXTRA] = field(f, slice(MARGIN, MARGIN + EXTRA), wide)

    def copy(source, target, number, where):
        return pltpu.make_async_remote_copy(
            src_ref=source,
            dst_ref=target,
            send_sem=send_sem.at[number],
            recv_sem=recv_sem.at[number],
            device_id=where,
            device_id_type=MESH,
        )

    to_right = copy(x_out.at[0], x_in.at[0], 0, {"gx": right})
    to_left = copy(x_out.at[1], x_in.at[1], 1, {"gx": left})
    to_lower = copy(y_up, in_hi, 2, {"gy": lower})
    to_upper = copy(y_dn, in_lo, 3, {"gy": upper})
    corner_lower = copy(c_up, cin_hi, 4, {"gy": lower})
    corner_upper = copy(c_dn, cin_lo, 5, {"gy": upper})

    pl.semaphore_wait(barrier, 2 + has_lo.astype(jnp.int32) + has_hi.astype(jnp.int32))
    to_right.start()
    to_left.start()

    @pl.when(has_lo)
    def _():
        to_lower.start()

    @pl.when(has_hi)
    def _():
        to_upper.start()

    to_right.wait_recv()
    to_left.wait_recv()
    for f in range(FIELDS):
        tile, at = f // PER_TILE, (f % PER_TILE) * WIDE
        from_right = rolled(x_in[1, tile], -at)
        from_left = rolled(x_in[0, tile], LANES - WIDE - at)
        halo[f, MARGIN : MARGIN + rows] = jnp.where(
            lanes < WIDE, from_right, jnp.where(lanes >= LANES - WIDE, from_left, 0.0)
        )

    def packed(start, count, tile):
        index = lane_index(count)
        total = jnp.zeros((count, LANES), jnp.float32)
        for f in range(tile * PER_CORNER, min(FIELDS, (tile + 1) * PER_CORNER)):
            at = (f - tile * PER_CORNER) * 2 * WIDE
            here = jnp.logical_and(index >= at, index < at + 2 * WIDE)
            total = jnp.where(here, rolled(halo[f, start : start + count], WIDE + at), total)
        return total

    for tile in range(C_TILES):
        at = slice(tile * MARGIN, (tile + 1) * MARGIN)
        c_up[at] = packed(MARGIN, MARGIN, tile)
        c_dn[at] = packed(rows, MARGIN, tile)
    c_up[C_TILES * MARGIN :] = packed(2 * MARGIN, EXTRA, 0)

    @pl.when(has_lo)
    def _():
        corner_lower.start()

    @pl.when(has_hi)
    def _():
        corner_upper.start()

    def unpacked(source, start, count, f):
        index = lane_index(count)
        value = rolled(source[start : start + count], -(WIDE + (f % PER_CORNER) * 2 * WIDE))
        return jnp.where(jnp.logical_or(index < WIDE, index >= LANES - WIDE), value, 0.0)

    @pl.when(has_lo)
    def _():
        to_upper.wait_recv()
        rows_lo[...] = in_lo[...]
        corner_upper.wait_recv()
        for f in range(FIELDS):
            halo[f, 0:MARGIN] = unpacked(cin_lo, f // PER_CORNER * MARGIN, MARGIN, f)

    @pl.when(jnp.logical_not(has_lo))
    def _():
        rows_lo[...] = jnp.zeros_like(rows_lo)
        for f in range(FIELDS):
            halo[f, 0:MARGIN] = jnp.zeros((MARGIN, LANES), jnp.float32)

    high = MARGIN + rows

    @pl.when(has_hi)
    def _():
        to_lower.wait_recv()
        rows_hi[...] = in_hi[...]
        corner_lower.wait_recv()
        for f in range(FIELDS):
            halo[f, high : high + MARGIN] = unpacked(cin_hi, f // PER_CORNER * MARGIN, MARGIN, f)
        for f in range(2):
            halo[f, high + MARGIN :] = unpacked(cin_hi, C_TILES * MARGIN, EXTRA, f)

    @pl.when(jnp.logical_not(has_hi))
    def _():
        rows_hi[...] = jnp.zeros_like(rows_hi)
        for f in range(FIELDS):
            halo[f, high : high + MARGIN] = jnp.zeros((MARGIN, LANES), jnp.float32)
        for f in range(2):
            halo[f, high + MARGIN :] = jnp.zeros((EXTRA, LANES), jnp.float32)

    for f in range(2, FIELDS):
        halo[f, high + MARGIN :] = jnp.zeros((EXTRA, LANES), jnp.float32)

    to_right.wait_send()
    to_left.wait_send()

    @pl.when(has_lo)
    def _():
        to_lower.wait_send()
        corner_lower.wait_send()

    @pl.when(has_hi)
    def _():
        to_upper.wait_send()
        corner_upper.wait_send()


def subcycle_kernel(
    gy_count,
    vel, stress, derived, conc, mass, wind, cur, halo, rows_lo, rows_hi,
    vel_out, stress_out, newconc,
    east, north, plus, minus, twice, pressure, inertia, turning,
    wind_e, wind_n, cur_e, cur_n, active,
):
    rows, cols = conc.shape
    main = cols // LANES
    tiles = main + 1
    low, mid, high = TOP, TOP + MARGIN, TOP + MARGIN + rows
    total = high + MARGIN + EXTRA
    gy = lax.axis_index("gy")

    def raw(f, r, c):
        if f < 2:
            return vel[f, r, c]
        if f < 5:
            return stress[f - 2, r, c]
        if f == 5:
            return derived[0, r, c]
        if f == 6:
            return mass[r, c]
        if f < 9:
            return wind[f - 7, r, c]
        if f < 11:
            return cur[f - 9, r, c]
        return derived[1, r, c]

    def piece(f, part, tile):
        if tile == main:
            bounds = (0, MARGIN, MARGIN + rows, 2 * MARGIN + rows, 2 * MARGIN + rows + EXTRA)
            return halo[f, bounds[part] : bounds[part + 1], :]
        c = slice(tile * LANES, (tile + 1) * LANES)
        if part == 0:
            return rows_lo[f * MARGIN : (f + 1) * MARGIN, c]
        if part == 1:
            return raw(f, slice(0, rows), c)
        if part == 2:
            return rows_hi[f * MARGIN : (f + 1) * MARGIN, c]
        start = FIELDS * MARGIN + f * EXTRA
        return rows_hi[start : start + EXTRA, c]

    spans = ((low, MARGIN), (mid, rows), (high, MARGIN))
    for tile in range(tiles):
        for part, (start, count) in enumerate(spans):
            at = slice(start, start + count)
            alive = piece(11, part, tile)
            active[tile, at] = alive
            east[tile, at] = piece(0, part, tile) * alive
            north[tile, at] = piece(1, part, tile) * alive
            one, two = piece(2, part, tile), piece(3, part, tile)
            plus[tile, at] = one + two
            minus[tile, at] = one - two
            twice[tile, at] = 2.0 * piece(4, part, tile)
            pressure[tile, at] = (RELAX_RATE * 0.5 / (1.0 + RELAX_RATE)) * piece(5, part, tile)
            heavy = piece(6, part, tile)
            heavy = jnp.where(heavy == 0.0, 1.0, heavy)
            inertia[tile, at] = heavy / TIME_STEP
            row = lax.broadcasted_iota(jnp.int32, (count, LANES), 0) + (gy * rows + (start - mid))
            coriolis = CORIOLIS_TOP * (row.astype(jnp.float32) + 0.5) / (rows * gy_count)
            turning[tile, at] = coriolis * heavy
            wind_e[tile, at] = piece(7, part, tile)
            wind_n[tile, at] = piece(8, part, tile)
            cur_e[tile, at] = piece(9, part, tile)
            cur_n[tile, at] = piece(10, part, tile)
        for ref in (plus, minus, twice):
            ref[tile, 0:low] = jnp.zeros((low, LANES), jnp.float32)
        east[tile, total - EXTRA : total] = piece(0, 3, tile)
        north[tile, total - EXTRA : total] = piece(1, 3, tile)

    lanes = lane_index(STEP)
    at_end, at_start = lanes == LANES - 1, lanes == 0

    def ahead(values):
        turned = [rolled(v, -1) for v in values]
        return [jnp.where(at_end, turned[(t + 1) % tiles], turned[t]) for t in range(tiles)]

    def behind(values):
        turned = [rolled(v, 1) for v in values]
        return [jnp.where(at_start, turned[t - 1], turned[t]) for t in range(tiles)]

    def gradients(start):
        add, sub, add_s, sub_s = [], [], [], []
        for t in range(tiles):
            u0, u1 = east[t, pl.ds(start, STEP)], east[t, pl.ds(start + 1, STEP)]
            v0, v1 = north[t, pl.ds(start, STEP)], north[t, pl.ds(start + 1, STEP)]
            a, b, c, d = u0 + u1, u1 - u0, v0 + v1, v1 - v0
            add.append(a + d)
            sub.append(a - d)
            add_s.append(b + c)
            sub_s.append(b - c)
        return add, sub, add_s, sub_s

    def stress_rows(start, growth):
        add, sub, add_s, sub_s = gradients(start)
        add_next, sub_next, shear_next = ahead(add), ahead(sub), ahead(add_s)
        for t in range(tiles):
            div = add_next[t] - sub[t]
            tension = sub_next[t] - add[t]
            shear = shear_next[t] + sub_s[t]
            square = div * div + (1.0 / ECCENTRICITY_SQUARED) * (tension * tension + shear * shear)
            inverse = lax.rsqrt(jnp.maximum(square, TINY))
            ratio = jnp.minimum(square * inverse, 1.0)
            force = pressure[t, pl.ds(start, STEP)] * growth
            weight = force * jnp.minimum(inverse, 1.0)
            quarter = weight * (1.0 / ECCENTRICITY_SQUARED)
            change = weight * div - force * ratio
            other = quarter * tension
            at = pl.ds(start, STEP)
            plus[t, at] = plus[t, at] + (change + other)
            minus[t, at] = minus[t, at] + (change - other)
            twice[t, at] = twice[t, at] + quarter * shear

    def velocity_rows(start, scale):
        at, before = pl.ds(start, STEP), pl.ds(start - 1, STEP)
        e_near, e_far, n_near, n_far = [], [], [], []
        for t in range(tiles):
            p1, p0 = plus[t, at], plus[t, before]
            m1, m0 = minus[t, at], minus[t, before]
            s1, s0 = twice[t, at], twice[t, before]
            a, d, b, e = p0 + p1, s1 - s0, s0 + s1, m1 - m0
            e_near.append(a + d)
            e_far.append(a - d)
            n_near.append(b + e)
            n_far.append(b - e)
        e_far, n_far = behind(e_far), behind(n_far)
        for t in range(tiles):
            force_e = (e_near[t] - e_far[t]) * scale
            force_n = (n_near[t] - n_far[t]) * scale
            u, v = east[t, at], north[t, at]
            ce, cn = cur_e[t, at], cur_n[t, at]
            de, dn = ce - u, cn - v
            square = de * de + dn * dn
            drag = square * lax.rsqrt(jnp.maximum(square, TINY))
            heavy, turn = inertia[t, at], turning[t, at]
            diag = heavy + drag
            re = heavy * u + force_e + wind_e[t, at] + drag * ce
            rn = heavy * v + force_n + wind_n[t, at] + drag * cn
            inverse = lax.rsqrt(diag * diag + turn * turn)
            inverse = active[t, at] * (inverse * inverse)
            east[t, at] = (diag * re + turn * rn) * inverse
            north[t, at] = (diag * rn - turn * re) * inverse

    blocks = (high + MARGIN - low) // STEP
    gain = 1.0 + RELAX_RATE

    def subcycle(number, carried):
        growth, scale = carried

        stress_rows(low, growth)

        def both(block, _):
            start = pl.multiple_of(low + block * STEP, 8)
            stress_rows(start, growth)
            velocity_rows(start - STEP, scale)
            return 0

        lax.fori_loop(1, blocks, both, 0)
        velocity_rows(low + (blocks - 1) * STEP, scale)
        return growth * gain, scale * (1.0 / gain)

    lax.fori_loop(
        0, SUBCYCLES, subcycle, (jnp.float32(gain), jnp.float32(0.25 / gain))
    )

    shrink = 0.5 * gain**-SUBCYCLES
    own = slice(mid, high)
    for t in range(main):
        c = slice(t * LANES, (t + 1) * LANES)
        vel_out[0, :, c] = east[t, own]
        vel_out[1, :, c] = north[t, own]
        stress_out[0, :, c] = (plus[t, own] + minus[t, own]) * shrink
        stress_out[1, :, c] = (plus[t, own] - minus[t, own]) * shrink
        stress_out[2, :, c] = twice[t, own] * shrink
    for block in range(rows // STEP):
        add, sub, _, _ = gradients(mid + block * STEP)
        add_next = ahead(add)
        at = slice(block * STEP, (block + 1) * STEP)
        for t in range(main):
            c = slice(t * LANES, (t + 1) * LANES)
            value = conc[at, c]
            newconc[at, c] = jnp.clip(value - value * (0.5 * (add_next[t] - sub[t])), 0.0, 1.0)


def ensemble_kernel(count, vel, newconc, mean, spread, land_vel, land_conc, send_sem, recv_sem):
    me = lax.axis_index("ens")
    share = newconc.shape[0] // count
    barrier = pltpu.get_barrier_semaphore()
    peers = [lax.rem(me + step, count) for step in range(1, count)]
    for peer in peers:
        pl.semaphore_signal(barrier, inc=1, device_id={"ens": peer}, device_id_type=MESH)
    pl.semaphore_wait(barrier, count - 1)
    copies = []
    for step, peer in enumerate(peers):
        at = pl.ds(pl.multiple_of(peer * share, 8), share)
        for kind, (source, target) in enumerate(
            ((vel.at[:, at], land_vel.at[step]), (newconc.at[at], land_conc.at[step]))
        ):
            each = pltpu.make_async_remote_copy(
                src_ref=source,
                dst_ref=target,
                send_sem=send_sem.at[kind, step],
                recv_sem=recv_sem.at[kind, step],
                device_id={"ens": peer},
                device_id_type=MESH,
            )
            each.start()
            copies.append(each)
    for each in copies:
        each.wait_recv()
    at = pl.ds(pl.multiple_of(me * share, 8), share)
    for f in range(3):
        own = newconc[at] if f == 0 else vel[f - 1, at]
        values = [own]
        for step in range(count - 1):
            values.append(land_conc[step] if f == 0 else land_vel[step, f - 1])
        average = functools.reduce(jnp.add, values) / count
        mean[f] = average
        squares = [(value - average) * (value - average) for value in values]
        spread[f] = functools.reduce(jnp.add, squares) / count
    for each in copies:
        each.wait_send()


def solution(mesh):
    gx_count, gy_count, ens_count = mesh.shape["gx"], mesh.shape["gy"], mesh.shape["ens"]
    f32 = jnp.float32

    def vmem(*shape):
        return pltpu.VMEM(shape, f32)

    def specs(count):
        return [pl.BlockSpec(memory_space=pltpu.VMEM)] * count

    def body(velocity, stress, thickness, concentration, node_mass, wind, current, mask, ice):
        rows, cols = mask.shape
        vel, stress = velocity[0], stress[0]
        conc, mass, wind, current = concentration[0], node_mass[0], wind[0], current[0]
        up_rows, dn_rows = FIELDS * MARGIN + 2 * EXTRA, FIELDS * MARGIN
        cu_rows, cd_rows = C_TILES * MARGIN + EXTRA, C_TILES * MARGIN
        tall = rows + 2 * MARGIN + EXTRA
        shape = lambda *dims: jax.ShapeDtypeStruct(dims, f32)
        derived, halo, rows_lo, rows_hi = pl.pallas_call(
            functools.partial(exchange_kernel, (gx_count, gy_count)),
            name="halo_exchange",
            out_shape=(
                shape(2, rows, cols),
                shape(FIELDS, tall, LANES),
                shape(dn_rows, cols),
                shape(up_rows, cols),
            ),
            in_specs=specs(9),
            out_specs=tuple(specs(4)),
            scratch_shapes=[
                vmem(2, X_TILES, rows, LANES),
                vmem(2, X_TILES, rows, LANES),
                vmem(up_rows, cols),
                vmem(dn_rows, cols),
                vmem(up_rows, cols),
                vmem(dn_rows, cols),
                vmem(cu_rows, LANES),
                vmem(cd_rows, LANES),
                vmem(cu_rows, LANES),
                vmem(cd_rows, LANES),
                pltpu.SemaphoreType.DMA((6,)),
                pltpu.SemaphoreType.DMA((6,)),
            ],
            compiler_params=pltpu.CompilerParams(collective_id=0, has_side_effects=True),
        )(vel, stress, thickness[0], conc, mass, wind, current, mask, ice[0])
        tiles = cols // LANES + 1
        vel_out, stress_out, newconc = pl.pallas_call(
            functools.partial(subcycle_kernel, gy_count),
            name="subcycles",
            out_shape=(shape(2, rows, cols), shape(3, rows, cols), shape(rows, cols)),
            in_specs=specs(10),
            out_specs=tuple(specs(3)),
            scratch_shapes=[vmem(tiles, TOP + tall, LANES)] * 13,
        )(vel, stress, derived, conc, mass, wind, current, halo, rows_lo, rows_hi)
        share = rows // ens_count
        mean, spread = pl.pallas_call(
            functools.partial(ensemble_kernel, ens_count),
            name="ensemble",
            out_shape=(shape(3, share, cols), shape(3, share, cols)),
            in_specs=specs(2),
            out_specs=tuple(specs(2)),
            scratch_shapes=[
                vmem(ens_count - 1, 2, share, cols),
                vmem(ens_count - 1, share, cols),
                pltpu.SemaphoreType.DMA((2, ens_count - 1)),
                pltpu.SemaphoreType.DMA((2, ens_count - 1)),
            ],
            compiler_params=pltpu.CompilerParams(collective_id=1, has_side_effects=True),
        )(vel_out, newconc)
        return vel_out[None], stress_out[None], mean, spread

    grid = P("ens", "gy", "gx")
    pair = P("ens", None, "gy", "gx")
    split = P(None, ("gy", "ens"), "gx")
    return jax.shard_map(
        body,
        mesh=mesh,
        in_specs=(pair, pair, grid, grid, grid, pair, pair, P("gy", "gx"), grid),
        out_specs=(pair, pair, split, split),
        check_vma=False,
    )
```

profile of v0, /device:TPU:0, one launch (start us, length us, event | category | flops | bytes accessed | tf_op | source)
XLA Modules:
  0.0 70.6 jit_solution(4371874212881944672)
XLA Ops:
  0.6 17.6 %halo_exchange.1 = (f32[2,256,256]{2,1,0:T(8,128)}, f32[12,296,128]{2,1,0:T(8,128)}, f32[192,256]{1,0:T(8,128)}, f32[208,256]{1,0:T(8,128)}) custom-call(f32[2,256,256]{2,1,0:T(8,128)} %bitcast.12, f32[3,256,256]{2,1,0:T(8,128)} %bitcast.10, f32[256,256]{1,0:T(8,128)} %bitcast.23, f32[256,256]{1,0:T(8,128)} %bitcast.18, f32[256,256]{1,0:T(8,128)} %bitcast.20, ...), custom_call_target="tpu_custom_call" | custom-call | tf_op jit(solution)/shard_map/halo_exchange/pallas_call | solution.py:485
  18.3 35.5 %subcycles.1 = (f32[2,256,256]{2,1,0:T(8,128)}, f32[3,256,256]{2,1,0:T(8,128)}, f32[256,256]{1,0:T(8,128)}) custom-call(f32[2,256,256]{2,1,0:T(8,128)} %bitcast.13, f32[3,256,256]{2,1,0:T(8,128)} %bitcast.11, f32[2,256,256]{2,1,0:T(8,128)} %get-tuple-element.13.derived, f32[256,256]{1,0:T(8,128)} %bitcast.19, f32[256,256]{1,0:T(8,128)} %bitcast.21, ...), custom_call_target="tpu_custom_call" | custom-call | tf_op jit(solution)/shard_map/subcycles/pallas_call | solution.py:513
  53.7 13.3 %ensemble.1 = (f32[3,128,256]{2,1,0:T(8,128)}, f32[3,128,256]{2,1,0:T(8,128)}) custom-call(f32[2,256,256]{2,1,0:T(8,128)} %get-tuple-element.17.vel, f32[256,256]{1,0:T(8,128)} %get-tuple-element.19.newconc), custom_call_target="tpu_custom_call" | custom-call | tf_op jit(solution)/shard_map/ensemble/pallas_call | solution.py:522
  67.1 1.8 %copy.15 = f32[3,128,256]{2,1,0:T(8,128)} copy(f32[3,128,256]{2,1,0:T(8,128)} %get-tuple-element.28) | data formatting | bytes 786432
  68.8 1.8 %copy.16 = f32[3,128,256]{2,1,0:T(8,128)} copy(f32[3,128,256]{2,1,0:T(8,128)} %get-tuple-element.29) | data formatting | bytes 786432
where the time goes:
time: 70.8 us; the launch traced here: 70.6 us
  Pallas kernels  66.4 us (94%)
  local copies, waits for them, and re-layouts  3.53 us (5%)
    pallas_call x1, Pallas kernels, body(): pl.pallas_call(functools.partial(subcycle_kernel, gy_count), name='subcyc...  35.5 us
    pallas_call x1, Pallas kernels, body(): pl.pallas_call(functools.partial(exchange_kernel, (gx_count, gy_count)),...  17.6 us
    pallas_call x1, Pallas kernels, body(): pl.pallas_call(functools.partial(ensemble_kernel, ens_count), name='ensem...  13.3 us
    unnamed x2, local copies, waits for them, and re-layouts  3.53 us

commit v1 on v0

--- a/solution.py
+++ b/solution.py
@@ -242,7 +242,7 @@
 def subcycle_kernel(
     gy_count,
     vel, stress, derived, conc, mass, wind, cur, halo, rows_lo, rows_hi,
-    vel_out, stress_out, newconc,
+    vel_out, stress_out, fields,
     east, north, plus, minus, twice, pressure, inertia, turning,
     wind_e, wind_n, cur_e, cur_n, active,
 ):
@@ -409,8 +409,8 @@
     own = slice(mid, high)
     for t in range(main):
         c = slice(t * LANES, (t + 1) * LANES)
-        vel_out[0, :, c] = east[t, own]
-        vel_out[1, :, c] = north[t, own]
+        vel_out[0, :, c] = fields[1, :, c] = east[t, own]
+        vel_out[1, :, c] = fields[2, :, c] = north[t, own]
         stress_out[0, :, c] = (plus[t, own] + minus[t, own]) * shrink
         stress_out[1, :, c] = (plus[t, own] - minus[t, own]) * shrink
         stress_out[2, :, c] = twice[t, own] * shrink
@@ -421,12 +421,12 @@
         for t in range(main):
             c = slice(t * LANES, (t + 1) * LANES)
             value = conc[at, c]
-            newconc[at, c] = jnp.clip(value - value * (0.5 * (add_next[t] - sub[t])), 0.0, 1.0)
-
-
-def ensemble_kernel(count, vel, newconc, mean, spread, land_vel, land_conc, send_sem, recv_sem):
+            fields[0, at, c] = jnp.clip(value - value * (0.5 * (add_next[t] - sub[t])), 0.0, 1.0)
+
+
+def ensemble_kernel(count, fields, mean, spread, landing, send_sem, recv_sem):
     me = lax.axis_index("ens")
-    share = newconc.shape[0] // count
+    share = mean.shape[1]
     barrier = pltpu.get_barrier_semaphore()
     peers = [lax.rem(me + step, count) for step in range(1, count)]
     for peer in peers:
@@ -434,32 +434,23 @@
     pl.semaphore_wait(barrier, count - 1)
     copies = []
     for step, peer in enumerate(peers):
-        at = pl.ds(pl.multiple_of(peer * share, 8), share)
-        for kind, (source, target) in enumerate(
-            ((vel.at[:, at], land_vel.at[step]), (newconc.at[at], land_conc.at[step]))
-        ):
-            each = pltpu.make_async_remote_copy(
-                src_ref=source,
-                dst_ref=target,
-                send_sem=send_sem.at[kind, step],
-                recv_sem=recv_sem.at[kind, step],
-                device_id={"ens": peer},
-                device_id_type=MESH,
-            )
-            each.start()
-            copies.append(each)
+        each = pltpu.make_async_remote_copy(
+            src_ref=fields.at[:, pl.ds(pl.multiple_of(peer * share, 8), share)],
+            dst_ref=landing.at[step],
+            send_sem=send_sem.at[step],
+            recv_sem=recv_sem.at[step],
+            device_id={"ens": peer},
+            device_id_type=MESH,
+        )
+        each.start()
+        copies.append(each)
     for each in copies:
         each.wait_recv()
-    at = pl.ds(pl.multiple_of(me * share, 8), share)
-    for f in range(3):
-        own = newconc[at] if f == 0 else vel[f - 1, at]
-        values = [own]
-        for step in range(count - 1):
-            values.append(land_conc[step] if f == 0 else land_vel[step, f - 1])
-        average = functools.reduce(jnp.add, values) / count
-        mean[f] = average
-        squares = [(value - average) * (value - average) for value in values]
-        spread[f] = functools.reduce(jnp.add, squares) / count
+    own = fields[:, pl.ds(pl.multiple_of(me * share, 8), share)]
+    values = [own] + [landing[step] for step in range(count - 1)]
+    average = functools.reduce(jnp.add, values) / count
+    mean[...] = average
+    spread[...] = functools.reduce(jnp.add, [(v - average) * (v - average) for v in values]) / count
     for each in copies:
         each.wait_send()
 
@@ -507,32 +498,32 @@
                 pltpu.SemaphoreType.DMA((6,)),
                 pltpu.SemaphoreType.DMA((6,)),
             ],
-            compiler_params=pltpu.CompilerParams(collective_id=0, has_side_effects=True),
+            compiler_params=pltpu.CompilerParams(collective_id=0, has_side_effects=True, vmem_limit_bytes=16 << 20),
         )(vel, stress, thickness[0], conc, mass, wind, current, mask, ice[0])
         tiles = cols // LANES + 1
-        vel_out, stress_out, newconc = pl.pallas_call(
+        vel_out, stress_out, fields = pl.pallas_call(
             functools.partial(subcycle_kernel, gy_count),
             name="subcycles",
-            out_shape=(shape(2, rows, cols), shape(3, rows, cols), shape(rows, cols)),
+            out_shape=(shape(2, rows, cols), shape(3, rows, cols), shape(3, rows, cols)),
             in_specs=specs(10),
             out_specs=tuple(specs(3)),
             scratch_shapes=[vmem(tiles, TOP + tall, LANES)] * 13,
+            compiler_params=pltpu.CompilerParams(vmem_limit_bytes=20 << 20),
         )(vel, stress, derived, conc, mass, wind, current, halo, rows_lo, rows_hi)
         share = rows // ens_count
         mean, spread = pl.pallas_call(
             functools.partial(ensemble_kernel, ens_count),
             name="ensemble",
             out_shape=(shape(3, share, cols), shape(3, share, cols)),
-            in_specs=specs(2),
+            in_specs=specs(1),
             out_specs=tuple(specs(2)),
             scratch_shapes=[
-                vmem(ens_count - 1, 2, share, cols),
-                vmem(ens_count - 1, share, cols),
-                pltpu.SemaphoreType.DMA((2, ens_count - 1)),
-                pltpu.SemaphoreType.DMA((2, ens_count - 1)),
+                vmem(ens_count - 1, 3, share, cols),
+                pltpu.SemaphoreType.DMA((ens_count - 1,)),
+                pltpu.SemaphoreType.DMA((ens_count - 1,)),
             ],
-            compiler_params=pltpu.CompilerParams(collective_id=1, has_side_effects=True),
-        )(vel_out, newconc)
+            compiler_params=pltpu.CompilerParams(collective_id=1, has_side_effects=True, vmem_limit_bytes=6 << 20),
+        )(fields)
         return vel_out[None], stress_out[None], mean, spread
 
     grid = P("ens", "gy", "gx")

time: 70.8 us -> 69.3 us (0.979)
  Pallas kernels: 66.4 us -> 57.9 us
  local copies, waits for them, and re-layouts: 3.53 us -> 10.3 us
    unnamed x2 -> x32, local copies, waits for them, and re-layouts: 3.53 us -> 10.3 us
    pallas_call x1, Pallas kernels: 17.6 us -> 14.2 us  [body(): pl.pallas_call(functools.partial(exchange_kernel, (gx_count, gy_count)),...]
    pallas_call x1, Pallas kernels: 35.5 us -> 32.4 us  [body(): pl.pallas_call(functools.partial(subcycle_kernel, gy_count), name='subcyc...]
    pallas_call x1, Pallas kernels: 13.3 us -> 11.3 us  [body(): pl.pallas_call(functools.partial(ensemble_kernel, ens_count), name='ensem...]
where the time goes in v1:
time: 69.3 us; the launch traced here: 68.9 us
  Pallas kernels  57.9 us (84%)
  local copies, waits for them, and re-layouts  10.3 us (15%)
  between operations  0.74 us (1%)
    pallas_call x1, Pallas kernels, body(): pl.pallas_call(functools.partial(subcycle_kernel, gy_count), name='subcyc...  32.4 us
    pallas_call x1, Pallas kernels, body(): pl.pallas_call(functools.partial(exchange_kernel, (gx_count, gy_count)),...  14.2 us
    pallas_call x1, Pallas kernels, body(): pl.pallas_call(functools.partial(ensemble_kernel, ens_count), name='ensem...  11.3 us
    unnamed x32, local copies, waits for them, and re-layouts  10.3 us

profile of v1, /device:TPU:0, one launch (start us, length us, event | category | flops | bytes accessed | tf_op | source)
XLA Modules:
  0.0 68.9 jit_solution(11808443362697481539)
XLA Ops:
  0.6 0.0 copy-start
  0.6 1.1 %copy-done = f32[1,3,256,256]{3,2,1,0:T(8,128)S(1)} copy-done((f32[1,3,256,256]{3,2,1,0:T(8,128)S(1)}, f32[1,3,256,256]{3,2,1,0:T(8,128)}, u32[]{:S(2)}) %copy-start) | copy-done | bytes 786456
  1.8 0.0 copy-start.2
  1.8 1.0 %copy-done.2 = f32[1,2,256,256]{3,2,1,0:T(8,128)S(1)} copy-done((f32[1,2,256,256]{3,2,1,0:T(8,128)S(1)}, f32[1,2,256,256]{3,2,1,0:T(8,128)}, u32[]{:S(2)}) %copy-start.2) | copy-done | bytes 524312
  2.8 0.0 copy-start.4
  2.8 1.0 %copy-done.4 = f32[1,2,256,256]{3,2,1,0:T(8,128)S(1)} copy-done((f32[1,2,256,256]{3,2,1,0:T(8,128)S(1)}, f32[1,2,256,256]{3,2,1,0:T(8,128)}, u32[]{:S(2)}) %copy-start.4) | copy-done | bytes 524312
  3.9 0.0 copy-start.6
  3.9 1.0 %copy-done.6 = f32[1,2,256,256]{3,2,1,0:T(8,128)S(1)} copy-done((f32[1,2,256,256]{3,2,1,0:T(8,128)S(1)}, f32[1,2,256,256]{3,2,1,0:T(8,128)}, u32[]{:S(2)}) %copy-start.6) | copy-done | bytes 524312
  4.9 0.0 copy-start.8
  4.9 0.9 %copy-done.8 = f32[1,256,256]{2,1,0:T(8,128)S(1)} copy-done((f32[1,256,256]{2,1,0:T(8,128)S(1)}, f32[1,256,256]{2,1,0:T(8,128)}, u32[]{:S(2)}) %copy-start.8) | copy-done | bytes 262168
  5.8 0.0 copy-start.10
  5.8 0.9 %copy-done.10 = f32[1,256,256]{2,1,0:T(8,128)S(1)} copy-done((f32[1,256,256]{2,1,0:T(8,128)S(1)}, f32[1,256,256]{2,1,0:T(8,128)}, u32[]{:S(2)}) %copy-start.10) | copy-done | bytes 262168
  6.8 0.0 copy-start.12
  6.8 0.9 %copy-done.12 = f32[1,256,256]{2,1,0:T(8,128)S(1)} copy-done((f32[1,256,256]{2,1,0:T(8,128)S(1)}, f32[1,256,256]{2,1,0:T(8,128)}, u32[]{:S(2)}) %copy-start.12) | copy-done | bytes 262168
  7.7 0.0 copy-start.13
  7.7 0.9 %copy-done.13 = s32[256,256]{1,0:T(8,128)S(1)} copy-done((s32[256,256]{1,0:T(8,128)S(1)}, s32[256,256]{1,0:T(8,128)}, u32[]{:S(2)}) %copy-start.13) | copy-done | bytes 262168
  8.7 0.0 copy-start.14
  8.7 0.7 copy-done.14
  9.4 0.0 copy-start.1
  9.4 0.0 copy-start.3
  9.4 0.0 copy-start.5
  9.4 0.0 copy-start.7
  9.4 0.0 copy-start.9
  9.4 0.0 copy-start.11
  9.4 14.2 %halo_exchange.1 = (f32[2,256,256]{2,1,0:T(8,128)S(1)}, f32[12,296,128]{2,1,0:T(8,128)S(1)}, f32[192,256]{1,0:T(8,128)S(1)}, f32[208,256]{1,0:T(8,128)S(1)}) custom-call(f32[2,256,256]{2,1,0:T(8,128)S(1)} %bitcast.12, f32[3,256,256]{2,1,0:T(8,128)S(1)} %bitcast.10, f32[256,256]{1,0:T(8,128)S(1)} %bitcast.22, f32[256,256]{1,0:T(8,128)S(1)} %bitcast.18, ...), custom_call_target="tpu_custom_call" | custom-call | tf_op jit(solution)/shard_map/halo_exchange/pallas_call | solution.py:476
  23.6 0.0 copy-done.1
  23.6 0.0 copy-done.3
  23.6 0.0 copy-done.5
  23.6 0.0 copy-done.7
  23.6 0.0 copy-done.9
  23.7 0.0 copy-done.11
  23.7 32.4 %subcycles.1 = (f32[2,256,256]{2,1,0:T(8,128)}, f32[3,256,256]{2,1,0:T(8,128)}, f32[3,256,256]{2,1,0:T(8,128)S(1)}) custom-call(f32[2,256,256]{2,1,0:T(8,128)S(1)} %bitcast.13, f32[3,256,256]{2,1,0:T(8,128)S(1)} %bitcast.11, f32[2,256,256]{2,1,0:T(8,128)S(1)} %get-tuple-element.13.derived, f32[256,256]{1,0:T(8,128)S(1)} %bitcast.19, ...), custom_call_target="tpu_custom_call" | custom-call | tf_op jit(solution)/shard_map/subcycles/pallas_call | solution.py:504
  56.1 11.3 %ensemble.1 = (f32[3,128,256]{2,1,0:T(8,128)S(1)}, f32[3,128,256]{2,1,0:T(8,128)S(1)}) custom-call(f32[3,256,256]{2,1,0:T(8,128)S(1)} %get-tuple-element.19.fields), custom_call_target="tpu_custom_call" | custom-call | tf_op jit(solution)/shard_map/ensemble/pallas_call | solution.py:514
  67.4 0.7 %copy.15 = f32[3,128,256]{2,1,0:T(8,128)} copy(f32[3,128,256]{2,1,0:T(8,128)S(1)} %get-tuple-element.28) | data formatting | bytes 786432
  68.1 0.7 %copy.16 = f32[3,128,256]{2,1,0:T(8,128)} copy(f32[3,128,256]{2,1,0:T(8,128)S(1)} %get-tuple-element.29) | data formatting | bytes 786432
Async XLA Ops:
  0.6 1.1 %copy-start = (f32[1,3,256,256]{3,2,1,0:T(8,128)S(1)}, f32[1,3,256,256]{3,2,1,0:T(8,128)}, u32[]{:S(2)}) copy-start(f32[1,3,256,256]{3,2,1,0:T(8,128)} %param.10) | copy-start | bytes 2359300
  1.8 1.0 %copy-start.2 = (f32[1,2,256,256]{3,2,1,0:T(8,128)S(1)}, f32[1,2,256,256]{3,2,1,0:T(8,128)}, u32[]{:S(2)}) copy-start(f32[1,2,256,256]{3,2,1,0:T(8,128)} %param.9) | copy-start | bytes 1572868
  2.8 1.0 %copy-start.4 = (f32[1,2,256,256]{3,2,1,0:T(8,128)S(1)}, f32[1,2,256,256]{3,2,1,0:T(8,128)}, u32[]{:S(2)}) copy-start(f32[1,2,256,256]{3,2,1,0:T(8,128)} %param.14) | copy-start | bytes 1572868
  3.9 1.0 %copy-start.6 = (f32[1,2,256,256]{3,2,1,0:T(8,128)S(1)}, f32[1,2,256,256]{3,2,1,0:T(8,128)}, u32[]{:S(2)}) copy-start(f32[1,2,256,256]{3,2,1,0:T(8,128)} %param.15) | copy-start | bytes 1572868
  4.9 0.9 %copy-start.8 = (f32[1,256,256]{2,1,0:T(8,128)S(1)}, f32[1,256,256]{2,1,0:T(8,128)}, u32[]{:S(2)}) copy-start(f32[1,256,256]{2,1,0:T(8,128)} %param.12) | copy-start | bytes 786436
  5.8 0.9 %copy-start.10 = (f32[1,256,256]{2,1,0:T(8,128)S(1)}, f32[1,256,256]{2,1,0:T(8,128)}, u32[]{:S(2)}) copy-start(f32[1,256,256]{2,1,0:T(8,128)} %param.13) | copy-start | bytes 786436
  6.8 0.9 %copy-start.12 = (f32[1,256,256]{2,1,0:T(8,128)S(1)}, f32[1,256,256]{2,1,0:T(8,128)}, u32[]{:S(2)}) copy-start(f32[1,256,256]{2,1,0:T(8,128)} %param.11) | copy-start | bytes 786436
  7.7 0.9 %copy-start.13 = (s32[256,256]{1,0:T(8,128)S(1)}, s32[256,256]{1,0:T(8,128)}, u32[]{:S(2)}) copy-start(s32[256,256]{1,0:T(8,128)} %mask.1) | copy-start | bytes 786436
  8.7 0.7 copy-start.14
  9.4 14.2 %copy-start.1 = (f32[1,3,256,256]{3,2,1,0:T(8,128)S(1)}, f32[1,3,256,256]{3,2,1,0:T(8,128)}, u32[]{:S(2)}) copy-start(f32[1,3,256,256]{3,2,1,0:T(8,128)} %param.10) | copy-start | bytes 2359300
  9.4 14.2 %copy-start.3 = (f32[1,2,256,256]{3,2,1,0:T(8,128)S(1)}, f32[1,2,256,256]{3,2,1,0:T(8,128)}, u32[]{:S(2)}) copy-start(f32[1,2,256,256]{3,2,1,0:T(8,128)} %param.9) | copy-start | bytes 1572868
  9.4 14.2 %copy-start.5 = (f32[1,2,256,256]{3,2,1,0:T(8,128)S(1)}, f32[1,2,256,256]{3,2,1,0:T(8,128)}, u32[]{:S(2)}) copy-start(f32[1,2,256,256]{3,2,1,0:T(8,128)} %param.14) | copy-start | bytes 1572868
  9.4 14.2 %copy-start.7 = (f32[1,2,256,256]{3,2,1,0:T(8,128)S(1)}, f32[1,2,256,256]{3,2,1,0:T(8,128)}, u32[]{:S(2)}) copy-start(f32[1,2,256,256]{3,2,1,0:T(8,128)} %param.15) | copy-start | bytes 1572868
  9.4 14.3 %copy-start.9 = (f32[1,256,256]{2,1,0:T(8,128)S(1)}, f32[1,256,256]{2,1,0:T(8,128)}, u32[]{:S(2)}) copy-start(f32[1,256,256]{2,1,0:T(8,128)} %param.12) | copy-start | bytes 786436
  9.4 14.3 %copy-start.11 = (f32[1,256,256]{2,1,0:T(8,128)S(1)}, f32[1,256,256]{2,1,0:T(8,128)}, u32[]{:S(2)}) copy-start(f32[1,256,256]{2,1,0:T(8,128)} %param.13) | copy-start | bytes 786436

commit v2 on v1

--- a/solution.py
+++ b/solution.py
@@ -112,15 +112,6 @@
             west = jnp.where(here, rolled(field(f, every, first), at), west)
         x_out[0, tile] = east
         x_out[1, tile] = west
-    wide = slice(0, cols)
-    for f in range(FIELDS):
-        at = slice(f * MARGIN, (f + 1) * MARGIN)
-        y_up[at] = field(f, slice(0, MARGIN), wide)
-        y_dn[at] = field(f, slice(rows - MARGIN, rows), wide)
-    for f in range(2):
-        at = FIELDS * MARGIN + f * EXTRA
-        y_up[at : at + EXTRA] = field(f, slice(MARGIN, MARGIN + EXTRA), wide)
-
     def copy(source, target, number, where):
         return pltpu.make_async_remote_copy(
             src_ref=source,
@@ -141,6 +132,15 @@
     pl.semaphore_wait(barrier, 2 + has_lo.astype(jnp.int32) + has_hi.astype(jnp.int32))
     to_right.start()
     to_left.start()
+
+    wide = slice(0, cols)
+    for f in range(FIELDS):
+        at = slice(f * MARGIN, (f + 1) * MARGIN)
+        y_up[at] = field(f, slice(0, MARGIN), wide)
+        y_dn[at] = field(f, slice(rows - MARGIN, rows), wide)
+    for f in range(2):
+        at = FIELDS * MARGIN + f * EXTRA
+        y_up[at : at + EXTRA] = field(f, slice(MARGIN, MARGIN + EXTRA), wide)
 
     @pl.when(has_lo)
     def _():

time: 69.3 us -> 69.3 us (level)
  no operation moved by 1% of the time
where the time goes in v2:
time: 69.3 us; the launch traced here: 68.9 us
  Pallas kernels  57.9 us (84%)
  local copies, waits for them, and re-layouts  10.3 us (15%)
  between operations  0.74 us (1%)
    pallas_call x1, Pallas kernels, body(): pl.pallas_call(functools.partial(subcycle_kernel, gy_count), name='subcyc...  32.4 us
    pallas_call x1, Pallas kernels, body(): pl.pallas_call(functools.partial(exchange_kernel, (gx_count, gy_count)),...  14.2 us
    pallas_call x1, Pallas kernels, body(): pl.pallas_call(functools.partial(ensemble_kernel, ens_count), name='ensem...  11.3 us
    unnamed x32, local copies, waits for them, and re-layouts  10.3 us

profile of v2, /device:TPU:0, one launch (start us, length us, event | category | flops | bytes accessed | tf_op | source)
XLA Modules:
  0.0 68.9 jit_solution(8264922735590862259)
XLA Ops:
  0.6 0.0 copy-start
  0.6 1.1 %copy-done = f32[1,3,256,256]{3,2,1,0:T(8,128)S(1)} copy-done((f32[1,3,256,256]{3,2,1,0:T(8,128)S(1)}, f32[1,3,256,256]{3,2,1,0:T(8,128)}, u32[]{:S(2)}) %copy-start) | copy-done | bytes 786456
  1.8 0.0 copy-start.2
  1.8 1.0 %copy-done.2 = f32[1,2,256,256]{3,2,1,0:T(8,128)S(1)} copy-done((f32[1,2,256,256]{3,2,1,0:T(8,128)S(1)}, f32[1,2,256,256]{3,2,1,0:T(8,128)}, u32[]{:S(2)}) %copy-start.2) | copy-done | bytes 524312
  2.8 0.0 copy-start.4
  2.8 1.0 %copy-done.4 = f32[1,2,256,256]{3,2,1,0:T(8,128)S(1)} copy-done((f32[1,2,256,256]{3,2,1,0:T(8,128)S(1)}, f32[1,2,256,256]{3,2,1,0:T(8,128)}, u32[]{:S(2)}) %copy-start.4) | copy-done | bytes 524312
  3.9 0.0 copy-start.6
  3.9 1.0 %copy-done.6 = f32[1,2,256,256]{3,2,1,0:T(8,128)S(1)} copy-done((f32[1,2,256,256]{3,2,1,0:T(8,128)S(1)}, f32[1,2,256,256]{3,2,1,0:T(8,128)}, u32[]{:S(2)}) %copy-start.6) | copy-done | bytes 524312
  4.9 0.0 copy-start.8
  4.9 0.9 %copy-done.8 = f32[1,256,256]{2,1,0:T(8,128)S(1)} copy-done((f32[1,256,256]{2,1,0:T(8,128)S(1)}, f32[1,256,256]{2,1,0:T(8,128)}, u32[]{:S(2)}) %copy-start.8) | copy-done | bytes 262168
  5.8 0.0 copy-start.10
  5.8 0.9 %copy-done.10 = f32[1,256,256]{2,1,0:T(8,128)S(1)} copy-done((f32[1,256,256]{2,1,0:T(8,128)S(1)}, f32[1,256,256]{2,1,0:T(8,128)}, u32[]{:S(2)}) %copy-start.10) | copy-done | bytes 262168
  6.8 0.0 copy-start.12
  6.8 0.9 %copy-done.12 = f32[1,256,256]{2,1,0:T(8,128)S(1)} copy-done((f32[1,256,256]{2,1,0:T(8,128)S(1)}, f32[1,256,256]{2,1,0:T(8,128)}, u32[]{:S(2)}) %copy-start.12) | copy-done | bytes 262168
  7.7 0.0 copy-start.13
  7.7 0.9 %copy-done.13 = s32[256,256]{1,0:T(8,128)S(1)} copy-done((s32[256,256]{1,0:T(8,128)S(1)}, s32[256,256]{1,0:T(8,128)}, u32[]{:S(2)}) %copy-start.13) | copy-done | bytes 262168
  8.7 0.0 copy-start.14
  8.7 0.7 copy-done.14
  9.4 0.0 copy-start.1
  9.4 0.0 copy-start.3
  9.4 0.0 copy-start.5
  9.4 0.0 copy-start.7
  9.4 0.0 copy-start.9
  9.4 0.0 copy-start.11
  9.4 14.2 %halo_exchange.1 = (f32[2,256,256]{2,1,0:T(8,128)S(1)}, f32[12,296,128]{2,1,0:T(8,128)S(1)}, f32[192,256]{1,0:T(8,128)S(1)}, f32[208,256]{1,0:T(8,128)S(1)}) custom-call(f32[2,256,256]{2,1,0:T(8,128)S(1)} %bitcast.12, f32[3,256,256]{2,1,0:T(8,128)S(1)} %bitcast.10, f32[256,256]{1,0:T(8,128)S(1)} %bitcast.22, f32[256,256]{1,0:T(8,128)S(1)} %bitcast.18, ...), custom_call_target="tpu_custom_call" | custom-call | tf_op jit(solution)/shard_map/halo_exchange/pallas_call | solution.py:476
  23.6 0.0 copy-done.1
  23.6 0.0 copy-done.3
  23.6 0.0 copy-done.5
  23.6 0.0 copy-done.7
  23.6 0.0 copy-done.9
  23.7 0.0 copy-done.11
  23.7 32.4 %subcycles.1 = (f32[2,256,256]{2,1,0:T(8,128)}, f32[3,256,256]{2,1,0:T(8,128)}, f32[3,256,256]{2,1,0:T(8,128)S(1)}) custom-call(f32[2,256,256]{2,1,0:T(8,128)S(1)} %bitcast.13, f32[3,256,256]{2,1,0:T(8,128)S(1)} %bitcast.11, f32[2,256,256]{2,1,0:T(8,128)S(1)} %get-tuple-element.13.derived, f32[256,256]{1,0:T(8,128)S(1)} %bitcast.19, ...), custom_call_target="tpu_custom_call" | custom-call | tf_op jit(solution)/shard_map/subcycles/pallas_call | solution.py:504
  56.1 11.3 %ensemble.1 = (f32[3,128,256]{2,1,0:T(8,128)S(1)}, f32[3,128,256]{2,1,0:T(8,128)S(1)}) custom-call(f32[3,256,256]{2,1,0:T(8,128)S(1)} %get-tuple-element.19.fields), custom_call_target="tpu_custom_call" | custom-call | tf_op jit(solution)/shard_map/ensemble/pallas_call | solution.py:514
  67.4 0.7 %copy.15 = f32[3,128,256]{2,1,0:T(8,128)} copy(f32[3,128,256]{2,1,0:T(8,128)S(1)} %get-tuple-element.28) | data formatting | bytes 786432
  68.1 0.7 %copy.16 = f32[3,128,256]{2,1,0:T(8,128)} copy(f32[3,128,256]{2,1,0:T(8,128)S(1)} %get-tuple-element.29) | data formatting | bytes 786432
Async XLA Ops:
  0.6 1.1 %copy-start = (f32[1,3,256,256]{3,2,1,0:T(8,128)S(1)}, f32[1,3,256,256]{3,2,1,0:T(8,128)}, u32[]{:S(2)}) copy-start(f32[1,3,256,256]{3,2,1,0:T(8,128)} %param.10) | copy-start | bytes 2359300
  1.8 1.0 %copy-start.2 = (f32[1,2,256,256]{3,2,1,0:T(8,128)S(1)}, f32[1,2,256,256]{3,2,1,0:T(8,128)}, u32[]{:S(2)}) copy-start(f32[1,2,256,256]{3,2,1,0:T(8,128)} %param.9) | copy-start | bytes 1572868
  2.8 1.0 %copy-start.4 = (f32[1,2,256,256]{3,2,1,0:T(8,128)S(1)}, f32[1,2,256,256]{3,2,1,0:T(8,128)}, u32[]{:S(2)}) copy-start(f32[1,2,256,256]{3,2,1,0:T(8,128)} %param.14) | copy-start | bytes 1572868
  3.9 1.0 %copy-start.6 = (f32[1,2,256,256]{3,2,1,0:T(8,128)S(1)}, f32[1,2,256,256]{3,2,1,0:T(8,128)}, u32[]{:S(2)}) copy-start(f32[1,2,256,256]{3,2,1,0:T(8,128)} %param.15) | copy-start | bytes 1572868
  4.9 0.9 %copy-start.8 = (f32[1,256,256]{2,1,0:T(8,128)S(1)}, f32[1,256,256]{2,1,0:T(8,128)}, u32[]{:S(2)}) copy-start(f32[1,256,256]{2,1,0:T(8,128)} %param.12) | copy-start | bytes 786436
  5.8 0.9 %copy-start.10 = (f32[1,256,256]{2,1,0:T(8,128)S(1)}, f32[1,256,256]{2,1,0:T(8,128)}, u32[]{:S(2)}) copy-start(f32[1,256,256]{2,1,0:T(8,128)} %param.13) | copy-start | bytes 786436
  6.8 0.9 %copy-start.12 = (f32[1,256,256]{2,1,0:T(8,128)S(1)}, f32[1,256,256]{2,1,0:T(8,128)}, u32[]{:S(2)}) copy-start(f32[1,256,256]{2,1,0:T(8,128)} %param.11) | copy-start | bytes 786436
  7.7 0.9 %copy-start.13 = (s32[256,256]{1,0:T(8,128)S(1)}, s32[256,256]{1,0:T(8,128)}, u32[]{:S(2)}) copy-start(s32[256,256]{1,0:T(8,128)} %mask.1) | copy-start | bytes 786436
  8.7 0.7 copy-start.14
  9.4 14.2 %copy-start.1 = (f32[1,3,256,256]{3,2,1,0:T(8,128)S(1)}, f32[1,3,256,256]{3,2,1,0:T(8,128)}, u32[]{:S(2)}) copy-start(f32[1,3,256,256]{3,2,1,0:T(8,128)} %param.10) | copy-start | bytes 2359300
  9.4 14.2 %copy-start.3 = (f32[1,2,256,256]{3,2,1,0:T(8,128)S(1)}, f32[1,2,256,256]{3,2,1,0:T(8,128)}, u32[]{:S(2)}) copy-start(f32[1,2,256,256]{3,2,1,0:T(8,128)} %param.9) | copy-start | bytes 1572868
  9.4 14.2 %copy-start.5 = (f32[1,2,256,256]{3,2,1,0:T(8,128)S(1)}, f32[1,2,256,256]{3,2,1,0:T(8,128)}, u32[]{:S(2)}) copy-start(f32[1,2,256,256]{3,2,1,0:T(8,128)} %param.14) | copy-start | bytes 1572868
  9.4 14.2 %copy-start.7 = (f32[1,2,256,256]{3,2,1,0:T(8,128)S(1)}, f32[1,2,256,256]{3,2,1,0:T(8,128)}, u32[]{:S(2)}) copy-start(f32[1,2,256,256]{3,2,1,0:T(8,128)} %param.15) | copy-start | bytes 1572868
  9.4 14.3 %copy-start.9 = (f32[1,256,256]{2,1,0:T(8,128)S(1)}, f32[1,256,256]{2,1,0:T(8,128)}, u32[]{:S(2)}) copy-start(f32[1,256,256]{2,1,0:T(8,128)} %param.12) | copy-start | bytes 786436
  9.4 14.3 %copy-start.11 = (f32[1,256,256]{2,1,0:T(8,128)S(1)}, f32[1,256,256]{2,1,0:T(8,128)}, u32[]{:S(2)}) copy-start(f32[1,256,256]{2,1,0:T(8,128)} %param.13) | copy-start | bytes 786436
